TPU v7x, 128 devices: a whole 4x4x4 slice. The times are simulated.
128 devices in a mesh: row: 8 (over z, y_lo), col: 16 (over x, y_hi, core).
Axes of the slice: x: 4, y: 4 (y_hi: 2, y_lo: 2; y = y_hi * 2 + y_lo), z: 4, core: 2. Of those that a mesh axis runs over, the one named last changes fastest.
Arguments:
- slab_pair: float32 [65536, 4096], P('row', 'col'), may hold values from -6 to 6, as said below
- butterfly_scale: float32 [65536], P('row'), may hold values from 0.5 to 2
Outputs:
- transformed: float32 [65536, 4096], P('row', 'col')
Inputs may be any that keep to these rules, and one draw needn't show every extreme that they name: The matrix is symmetric where the slab pair meets its own columns: with g(k) = k for k < 2048 and 32768 + k - 2048 otherwise, slab_pair[g(a), b] = slab_pair[g(b), a] for all a, b below 4096.
All inputs are finite; a program needn't handle non-finite values.
Results may differ from a plain program's by a relative error of at most 0.00002.
Values sent between devices are 32-bit elements; how exact they have to be, the bound alone decides.
A program may use at most 64 MiB of HBM per device.

v0:
```python
import jax
import jax.numpy as jnp
from jax import lax
from jax.sharding import PartitionSpec as P

N = 65536
W = 2048


def from_partner(block, axis, distance):
    count = lax.axis_size(axis)
    route = []
    for low in range(count):
        high = low | 1 << distance
        if high != low and high < count:
            route += [(low, high), (high, low)]
    return lax.ppermute(block, axis, route)


def row_pass(block_data, scale_here, is_top):
    row_bit = lax.axis_size("row").bit_length() - 2
    partner = from_partner(block_data, "row", row_bit)
    mixed = jnp.where(is_top, block_data + partner, partner - block_data)
    return mixed * scale_here[:, None] / jnp.float32(2.0) ** 0.5


def col_pass(block_data, col_scale, is_left):
    col_bit = lax.axis_size("col").bit_length() - 2
    partner = from_partner(block_data, "col", col_bit)
    mixed = jnp.where(is_left, block_data + partner, partner - block_data)
    return mixed * col_scale[None, :] / jnp.float32(2.0) ** 0.5


def per_device(slab_pair, butterfly_scale):
    row_count = lax.axis_size("row")
    col_count = lax.axis_size("col")
    row_here = lax.axis_index("row")
    col_here = lax.axis_index("col")
    local_rows = slab_pair.shape[0]
    local_cols = slab_pair.shape[1]
    is_top = row_here < row_count // 2
    is_left = col_here < col_count // 2
    gathered = lax.all_gather(butterfly_scale[:W], "row", axis=0, tiled=True)
    middle = row_count // 2 * W
    full_scale = jnp.concatenate([gathered[:W], gathered[middle : middle + W]])
    col_scale = lax.dynamic_slice_in_dim(full_scale, col_here * local_cols, local_cols, 0)
    mixed = col_pass(row_pass(slab_pair, butterfly_scale, is_top), col_scale, is_left)
    row_index = row_here * local_rows + jnp.arange(local_rows, dtype=jnp.int32)[:, None]
    col_index = col_here * local_cols + jnp.arange(local_cols, dtype=jnp.int32)[None, :]
    global_col = jnp.where(col_index < W, col_index, N // 2 + col_index - W)
    return jnp.where(row_index >= global_col, mixed, jnp.float32(0.0))


def solution(mesh):
    in_specs = (P("row", "col"), P("row"))
    out_specs = P("row", "col")
    return jax.shard_map(
        per_device, mesh=mesh, in_specs=in_specs, out_specs=out_specs, check_vma=False
    )
```

profile of v0, /device:TPU:6, one launch (start us, length us, event | category | flops | bytes accessed | tf_op | source)
XLA Modules:
  0.0 387.7 jit_solution(3690508631358408823)
XLA Ops:
  0.0 3.9 collective-permute-start
  3.9 0.0 slice-start
  3.9 180.8 %collective-permute-done = f32[8192,256]{1,0:T(8,128)} collective-permute-done((f32[8192,256]{1,0:T(8,128)}, f32[8192,256]{1,0:T(8,128)}, u32[]{:S(2)}, u32[]{:S(2)}) %collective-permute-start) | collective-permute-done | bytes 8388640 | tf_op jit(solution)/shard_map/ppermute | solution.py:17
  184.6 10.1 %multiply_multiply_fusion = f32[8192,256]{1,0:T(8,128)} fusion(f32[8192,256]{1,0:T(8,128)} %collective-permute-done, f32[8192,256]{1,0:T(8,128)} %param.2, f32[8192]{0:T(1024)} %param.3, pred[]{:T(512)S(6)} %lt.19), kind=kLoop, calls=%fused_computation.1 | loop fusion | flops 10485760 | bytes 25198592 | tf_op jit(solution)/shard_map/div | solution.py:24
  194.8 1.4 collective-permute-start.1
  196.2 0.0 slice-done
  196.2 29.0 %all_gather.3 = f32[16384]{0:T(1024)S(1)} all-gather(f32[2048]{0:T(1024)S(1)} %slice-done), channel_id=1, replica_groups=mesh['row'=8,'col'=16] {'row'}, dimensions={0}, use_global_device_ids=true | all-gather | bytes 73728 | tf_op jit(solution)/shard_map/all_gather | solution.py:43
  225.2 0.1 fusion
  225.3 152.9 %collective-permute-done.1 = f32[8192,256]{1,0:T(8,128)} collective-permute-done((f32[8192,256]{1,0:T(8,128)}, f32[8192,256]{1,0:T(8,128)}, u32[]{:S(2)}, u32[]{:S(2)}) %collective-permute-start.1) | collective-permute-done | bytes 8388640 | tf_op jit(solution)/shard_map/ppermute | solution.py:17
  378.2 9.5 %multiply_select_fusion = f32[8192,256]{1,0:T(8,128)} fusion(f32[8192,256]{1,0:T(8,128)} %collective-permute-done.1, f32[8192,256]{1,0:T(8,128)} %multiply_multiply_fusion, f32[256]{0:T(256)S(1)} %fusion, s32[256]{0:T(256)S(1)} %compare_select_fusion, s32[8192]{0:T(1024)S(1)} %iota_add_fusion, pred[]{:T(512)S(6)} %lt.18), kind=kLoop, calls=%fused_computation | loop fusion | flops 14680064 | bytes 25200640 | tf_op jit(solution)/shard_map/jit(_where)/select_n | solution.py:51
  (3 shorter events, 0.0 us)
Async XLA Ops:
  0.0 184.6 %collective-permute-start = (f32[8192,256]{1,0:T(8,128)}, f32[8192,256]{1,0:T(8,128)}, u32[]{:S(2)}, u32[]{:S(2)}) collective-permute-start(f32[8192,256]{1,0:T(8,128)} %param.2), channel_id=1, source_target_pairs={{0,64},{64,0},{16,80},{80,16},{32,96},{96,32},{48,112},{112,48},{1... | collective-permute-start | bytes 25165832 | tf_op jit(solution)/shard_map/ppermute | solution.py:17
  3.9 192.3 %slice-start = ((f32[8192]{0:T(1024)}), f32[2048]{0:T(1024)S(1)}, s32[]{:S(2)}) async-start(f32[8192]{0:T(1024)} %param.3), calls=%async_computation | async-start | bytes 16384 | tf_op jit(solution)/shard_map/slice | solution.py:43
  194.8 183.4 %collective-permute-start.1 = (f32[8192,256]{1,0:T(8,128)}, f32[8192,256]{1,0:T(8,128)}, u32[]{:S(2)}, u32[]{:S(2)}) collective-permute-start(f32[8192,256]{1,0:T(8,128)} %multiply_multiply_fusion), channel_id=1, source_target_pairs={{0,8},{8,0},{1,9},{9,1},{2,10},{10,2},{3,11},{11,3},{4,12},{12,4},... | collective-permute-start | bytes 25165832 | tf_op jit(solution)/shard_map/ppermute | solution.py:17
where the time goes:
time: 388 us
  waiting for transfers between devices  334 us (86%)
  blocking collectives  29 us (7%)
  other arithmetic  19.7 us (5%)
  starting transfers between devices  5.28 us (1%)
    ppermute x2, waiting for transfers between devices, from_partner(): return lax.ppermute(block, axis, route)  334 us
    all_gather x1, blocking collectives, per_device(): gathered = lax.all_gather(butterfly_scale[:W], 'row', axis=0, tiled=True)  29 us
    div x1, other arithmetic, row_pass(): return mixed * scale_here[:, None] / jnp.float32(2.0) ** 0.5  10.1 us
    select_n x1, other arithmetic, per_device(): return jnp.where(row_index >= global_col, mixed, jnp.float32(0.0))  9.48 us
  transfers between devices with their start and end apart: 2, of which 2 were waited for; matrix products, arithmetic and copies ran while one was open for 0% of the time, Pallas kernels for 0%

commit v1 on v0

v1 whole, which is shorter than its diff:
```python
import functools

import jax
import jax.numpy as jnp
from jax import lax
from jax.experimental import pallas as pl
from jax.experimental.pallas import tpu as pltpu
from jax.sharding import PartitionSpec as P

MESH = pl.DeviceIdType.MESH
N = 65536
W = 2048
CHUNK = 512
LANES = 128


def exchange_kernel(rows, cols, x_ref, s64_ref, s2_ref, out_ref,
                    mid, got1, got2, srow, cscale,
                    load_sem, send1, recv1, send2, recv2, cs_send, cs_recv):
    r = lax.axis_index("row")
    c = lax.axis_index("col")
    local_rows, local_cols = x_ref.shape
    count = local_rows // CHUNK
    half = count // 2
    top = r < rows // 2
    left = c < cols // 2
    z_peer = (lax.rem(r + rows // 2, rows), c)
    x_peer = (r, lax.rem(c + cols // 2, cols))
    source_row = jnp.where(left, 0, rows // 2)
    is_source = r == source_row

    barrier = pltpu.get_barrier_semaphore()
    pl.semaphore_signal(barrier, inc=1, device_id=z_peer, device_id_type=MESH)
    pl.semaphore_signal(barrier, inc=1, device_id=x_peer, device_id_type=MESH)

    @pl.when(jnp.logical_not(is_source))
    def _():
        pl.semaphore_signal(barrier, inc=1, device_id=(source_row, c), device_id_type=MESH)

    def window(i):
        return pl.ds(pl.multiple_of(i * CHUNK, CHUNK), CHUNK)

    def load(i):
        return pltpu.make_async_copy(x_ref.at[window(i)], mid.at[window(i)], load_sem.at[i])

    def first(i, peer):
        return pltpu.make_async_remote_copy(
            x_ref.at[window(i)], got1.at[window(i)], send1.at[i], recv1.at[i],
            device_id=peer, device_id_type=MESH)

    def second(i, peer):
        return pltpu.make_async_remote_copy(
            mid.at[window(i)], got2.at[window(i)], send2.at[i], recv2.at[i],
            device_id=peer, device_id_type=MESH)

    def scales(k):
        return pltpu.make_async_remote_copy(
            s2_ref.at[lax.rem(c, cols // 2)], cscale, cs_send.at[k], cs_recv,
            device_id=(lax.rem(source_row + 1 + k, rows), c), device_id_type=MESH)

    pl.semaphore_wait(barrier, jnp.where(is_source, 2 + rows - 1, 2))

    @pl.loop(0, half)
    def _(i):
        first(i, z_peer).start()
        first(i + half, x_peer).start()

    @pl.loop(0, count)
    def _(i):
        load(i).start()

    @pl.when(is_source)
    def _():
        cscale[...] = s2_ref[lax.rem(c, cols // 2)]

        @pl.loop(0, rows - 1)
        def _(k):
            scales(k).start()

    @pl.loop(0, local_rows // LANES)
    def _(g):
        line = jnp.broadcast_to(s64_ref[pl.ds(g, 1), :], (LANES, LANES))
        srow[pl.ds(pl.multiple_of(g * LANES, LANES), LANES), :] = line.T * jnp.float32(0.5)

    z_sign = jnp.where(top, 1.0, -1.0).astype(jnp.float32)
    x_sign = jnp.where(left, 1.0, -1.0).astype(jnp.float32)

    def mix(i, sign):
        mid[window(i), :] = got1[window(i), :] + sign * mid[window(i), :]

    @pl.loop(0, half)
    def _(i):
        load(i).wait()
        first(i, z_peer).wait_recv()
        mix(i, z_sign)
        second(i, x_peer).start()
        load(i + half).wait()
        first(i + half, x_peer).wait_recv()
        mix(i + half, x_sign)
        second(i + half, z_peer).start()

    @pl.when(is_source)
    def _():
        @pl.loop(0, rows - 1)
        def _(k):
            scales(k).wait_send()

    @pl.when(jnp.logical_not(is_source))
    def _():
        scales(0).wait_recv()

    global_col = jnp.where(left, c * local_cols, N // 2 + c * local_cols - W)

    def finish(i, sign):
        base = r * local_rows + i * CHUNK
        for b in range(local_cols // LANES):
            lanes = slice(b * LANES, (b + 1) * LANES)
            value = got2[window(i), lanes] + sign * mid[window(i), lanes]
            value = value * (srow[window(i), :] * cscale[b : b + 1, :])
            row_index = base + lax.broadcasted_iota(jnp.int32, (CHUNK, LANES), 0)
            col_index = global_col + b * LANES + lax.broadcasted_iota(jnp.int32, (CHUNK, LANES), 1)
            out_ref[window(i), lanes] = jnp.where(row_index >= col_index, value, jnp.float32(0.0))

    @pl.loop(0, half)
    def _(i):
        second(i, x_peer).wait_recv()
        finish(i, x_sign)
        second(i + half, z_peer).wait_recv()
        finish(i + half, z_sign)

    @pl.loop(0, half)
    def _(i):
        first(i, z_peer).wait_send()
        first(i + half, x_peer).wait_send()
        second(i, x_peer).wait_send()
        second(i + half, z_peer).wait_send()


def per_device(rows, cols, slab_pair, butterfly_scale):
    local_rows, local_cols = slab_pair.shape
    count = local_rows // CHUNK
    hbm = pl.BlockSpec(memory_space=pl.ANY)
    vmem = pl.BlockSpec(memory_space=pltpu.VMEM)
    s64 = butterfly_scale.reshape(local_rows // LANES, LANES)
    s2 = butterfly_scale.reshape(local_rows // local_cols, local_cols // LANES, LANES)
    block = pltpu.VMEM((local_rows, local_cols), jnp.float32)
    dma = pltpu.SemaphoreType.DMA
    return pl.pallas_call(
        functools.partial(exchange_kernel, rows, cols),
        out_shape=jax.ShapeDtypeStruct(slab_pair.shape, slab_pair.dtype),
        in_specs=[hbm, vmem, vmem],
        out_specs=vmem,
        scratch_shapes=[
            block, block, block,
            pltpu.VMEM((local_rows, LANES), jnp.float32),
            pltpu.VMEM((local_cols // LANES, LANES), jnp.float32),
            dma((count,)), dma((count,)), dma((count,)), dma((count,)), dma((count,)),
            dma((rows - 1,)), dma,
        ],
        compiler_params=pltpu.CompilerParams(
            collective_id=0, has_side_effects=True, vmem_limit_bytes=40 * 1024 * 1024
        ),
    )(slab_pair, s64, s2)


def solution(mesh):
    return jax.shard_map(
        functools.partial(per_device, mesh.shape["row"], mesh.shape["col"]),
        mesh=mesh,
        in_specs=(P("row", "col"), P("row")),
        out_specs=P("row", "col"),
        check_vma=False,
    )
```

time: 388 us -> 193 us (0.50)
  waiting for transfers between devices: 334 us -> 0 us
  Pallas kernels: 0 us -> 188 us
  blocking collectives: 29 us -> 0 us
  other arithmetic: 19.7 us -> 0 us
  starting transfers between devices: 5.28 us -> 0 us
  local copies, waits for them, and re-layouts: 0.01 us -> 4.16 us
    ppermute x2 -> x0, waiting for transfers between devices: 334 us -> none  [from_partner(): return lax.ppermute(block, axis, route)]
    pallas_call x0 -> x1, Pallas kernels: none -> 188 us  [per_device(): pl.pallas_call(functools.partial(exchange_kernel, rows, cols), out_shape=...]
    all_gather x1 -> x0, blocking collectives: 29 us -> none  [per_device(): gathered = lax.all_gather(butterfly_scale[:W], 'row', axis=0, tiled=True)]
    div x1 -> x0, other arithmetic: 10.1 us -> none  [row_pass(): return mixed * scale_here[:, None] / jnp.float32(2.0) ** 0.5]
    select_n x2 -> x0, other arithmetic: 9.48 us -> none  [the longest x1 9.48 us: per_device(): return jnp.where(row_index >= global_col, mixed, jnp.float32(0.0))]
    ppermute x2 -> x0, starting transfers between devices: 5.28 us -> none  [from_partner(): return lax.ppermute(block, axis, route)]
    unnamed x0 -> x3, local copies, waits for them, and re-layouts: none -> 4.16 us
  transfers between devices with their start and end apart: 2 -> 0, of which waited for: 2 -> 0; matrix products, arithmetic and copies ran while one was open for 0% -> 0% of each run, Pallas kernels for 0% -> 0%
where the time goes in v1:
time: 193 us; the launch traced here: 192 us
  Pallas kernels  188 us (97%)
  local copies, waits for them, and re-layouts  4.16 us (2%)
    pallas_call x1, Pallas kernels, per_device(): pl.pallas_call(functools.partial(exchange_kernel, rows, cols), out_shape=...  188 us
    unnamed x3, local copies, waits for them, and re-layouts  4.16 us

profile of v1, /device:TPU:6, one launch (start us, length us, event | category | flops | bytes accessed | tf_op | source)
XLA Modules:
  0.0 192.1 jit_solution(1883494974735480339)
XLA Ops:
  0.0 0.0 copy-start
  0.0 0.8 copy-done
  0.8 187.9 %shard_map.28 = f32[8192,256]{1,0:T(8,128)S(1)} custom-call(f32[8192,256]{1,0:T(8,128)} %x_ref.1, f32[64,128]{1,0:T(8,128)S(1)} %bitcast.2, f32[32,2,128]{2,1,0:T(2,128)S(1)} %bitcast.3), custom_call_target="tpu_custom_call" | custom-call | tf_op jit(solution)/shard_map/pallas_call | solution.py:148
  188.7 3.4 %copy.4 = f32[8192,256]{1,0:T(8,128)} copy(f32[8192,256]{1,0:T(8,128)S(1)} %shard_map.28) | data formatting | bytes 16777216
Async XLA Ops:
  0.0 0.8 copy-start

commit v2 on v1

--- a/solution.py
+++ b/solution.py
@@ -10,13 +10,14 @@
 MESH = pl.DeviceIdType.MESH
 N = 65536
 W = 2048
-CHUNK = 512
+CHUNK = 256
 LANES = 128
 
 
 def exchange_kernel(rows, cols, x_ref, s64_ref, s2_ref, out_ref,
-                    mid, got1, got2, srow, cscale,
-                    load_sem, send1, recv1, send2, recv2, cs_send, cs_recv):
+                    mid, got1, got2, srow, s64, cscale,
+                    load_sem, send1, recv1, send2, recv2, cs_send, cs_recv,
+                    scale_sem, ready_z, ready_x):
     r = lax.axis_index("row")
     c = lax.axis_index("col")
     local_rows, local_cols = x_ref.shape
@@ -29,14 +30,6 @@
     source_row = jnp.where(left, 0, rows // 2)
     is_source = r == source_row
 
-    barrier = pltpu.get_barrier_semaphore()
-    pl.semaphore_signal(barrier, inc=1, device_id=z_peer, device_id_type=MESH)
-    pl.semaphore_signal(barrier, inc=1, device_id=x_peer, device_id_type=MESH)
-
-    @pl.when(jnp.logical_not(is_source))
-    def _():
-        pl.semaphore_signal(barrier, inc=1, device_id=(source_row, c), device_id_type=MESH)
-
     def window(i):
         return pl.ds(pl.multiple_of(i * CHUNK, CHUNK), CHUNK)
 
@@ -55,32 +48,94 @@
 
     def scales(k):
         return pltpu.make_async_remote_copy(
-            s2_ref.at[lax.rem(c, cols // 2)], cscale, cs_send.at[k], cs_recv,
+            cscale, cscale, cs_send.at[k], cs_recv,
             device_id=(lax.rem(source_row + 1 + k, rows), c), device_id_type=MESH)
 
-    pl.semaphore_wait(barrier, jnp.where(is_source, 2 + rows - 1, 2))
-
-    @pl.loop(0, half)
-    def _(i):
-        first(i, z_peer).start()
-        first(i + half, x_peer).start()
+    barrier = pltpu.get_barrier_semaphore()
+
+    def greet(peer):
+        pl.semaphore_signal(barrier, inc=1, device_id=peer, device_id_type=MESH)
+
+    def answer(ready, peer):
+        pl.semaphore_signal(ready, inc=1, device_id=peer, device_id_type=MESH)
+
+    def send_z():
+        @pl.loop(0, half)
+        def _(i):
+            first(i, z_peer).start()
+
+    def send_x():
+        @pl.loop(half, count)
+        def _(i):
+            first(i, x_peer).start()
+
+    @pl.when(top)
+    def _():
+        greet(z_peer)
+
+    @pl.when(left)
+    def _():
+        greet(x_peer)
+
+    @pl.when(jnp.logical_not(is_source))
+    def _():
+        greet((source_row, c))
+
+    greetings = jnp.where(top, 0, 1) + jnp.where(left, 0, 1)
+
+    @pl.when(greetings > 0)
+    def _():
+        late_source = is_source & jnp.logical_not(left)
+        pl.semaphore_wait(barrier, greetings + jnp.where(late_source, rows - 1, 0))
+
+    @pl.when(jnp.logical_not(top))
+    def _():
+        answer(ready_z, z_peer)
+        send_z()
+
+    @pl.when(jnp.logical_not(left))
+    def _():
+        answer(ready_x, x_peer)
+        send_x()
+
+    @pl.when(top)
+    def _():
+        pl.semaphore_wait(ready_z, 1)
+        send_z()
+
+    @pl.when(left)
+    def _():
+        pl.semaphore_wait(ready_x, 1)
+        send_x()
+
+    load_scale = pltpu.make_async_copy(s64_ref, s64, scale_sem.at[0])
+    load_scale.start()
 
     @pl.loop(0, count)
     def _(i):
         load(i).start()
 
+    load_scale.wait()
+
+    @pl.loop(0, local_rows // LANES)
+    def _(g):
+        line = jnp.broadcast_to(s64[pl.ds(g, 1), :], (LANES, LANES))
+        srow[pl.ds(pl.multiple_of(g * LANES, LANES), LANES), :] = line.T * jnp.float32(0.5)
+
+    own_scale = pltpu.make_async_copy(s2_ref.at[lax.rem(c, cols // 2)], cscale, scale_sem.at[1])
+
     @pl.when(is_source)
     def _():
-        cscale[...] = s2_ref[lax.rem(c, cols // 2)]
+        own_scale.start()
+        own_scale.wait()
+
+        @pl.when(left)
+        def _():
+            pl.semaphore_wait(barrier, rows - 1)
 
         @pl.loop(0, rows - 1)
         def _(k):
             scales(k).start()
-
-    @pl.loop(0, local_rows // LANES)
-    def _(g):
-        line = jnp.broadcast_to(s64_ref[pl.ds(g, 1), :], (LANES, LANES))
-        srow[pl.ds(pl.multiple_of(g * LANES, LANES), LANES), :] = line.T * jnp.float32(0.5)
 
     z_sign = jnp.where(top, 1.0, -1.0).astype(jnp.float32)
     x_sign = jnp.where(left, 1.0, -1.0).astype(jnp.float32)
@@ -139,7 +194,7 @@
 def per_device(rows, cols, slab_pair, butterfly_scale):
     local_rows, local_cols = slab_pair.shape
     count = local_rows // CHUNK
-    hbm = pl.BlockSpec(memory_space=pl.ANY)
+    hbm = pl.BlockSpec(memory_space=pltpu.HBM)
     vmem = pl.BlockSpec(memory_space=pltpu.VMEM)
     s64 = butterfly_scale.reshape(local_rows // LANES, LANES)
     s2 = butterfly_scale.reshape(local_rows // local_cols, local_cols // LANES, LANES)
@@ -148,19 +203,21 @@
     return pl.pallas_call(
         functools.partial(exchange_kernel, rows, cols),
         out_shape=jax.ShapeDtypeStruct(slab_pair.shape, slab_pair.dtype),
-        in_specs=[hbm, vmem, vmem],
+        in_specs=[hbm, hbm, hbm],
         out_specs=vmem,
         scratch_shapes=[
             block, block, block,
             pltpu.VMEM((local_rows, LANES), jnp.float32),
+            pltpu.VMEM((local_rows // LANES, LANES), jnp.float32),
             pltpu.VMEM((local_cols // LANES, LANES), jnp.float32),
             dma((count,)), dma((count,)), dma((count,)), dma((count,)), dma((count,)),
-            dma((rows - 1,)), dma,
+            dma((rows - 1,)), dma, dma((2,)),
+            pltpu.SemaphoreType.REGULAR, pltpu.SemaphoreType.REGULAR,
         ],
         compiler_params=pltpu.CompilerParams(
             collective_id=0, has_side_effects=True, vmem_limit_bytes=40 * 1024 * 1024
         ),
-    )(slab_pair, s64, s2)
+    )(slab_pair, *(pltpu.with_memory_space_constraint(s, pltpu.HBM) for s in (s64, s2)))
 
 
 def solution(mesh):

time: 193 us -> 192 us (level)
    unnamed x3 -> x1, local copies, waits for them, and re-layouts: 4.16 us -> 3.4 us
where the time goes in v2:
time: 192 us
  Pallas kernels  189 us (98%)
  local copies, waits for them, and re-layouts  3.4 us (2%)
    pallas_call x1, Pallas kernels, per_device(): pl.pallas_call(functools.partial(exchange_kernel, rows, cols), out_shape=...  189 us

profile of v2, /device:TPU:6, one launch (start us, length us, event | category | flops | bytes accessed | tf_op | source)
XLA Modules:
  0.0 192.1 jit_solution(1372730679544983172)
XLA Ops:
  0.0 188.7 %shard_map.28 = f32[8192,256]{1,0:T(8,128)S(1)} custom-call(f32[8192,256]{1,0:T(8,128)} %x_ref.1, f32[64,128]{1,0:T(8,128)} %bitcast.2, f32[32,2,128]{2,1,0:T(2,128)} %bitcast.3), custom_call_target="tpu_custom_call" | custom-call | tf_op jit(solution)/shard_map/pallas_call | solution.py:203
  188.7 3.4 %copy.4 = f32[8192,256]{1,0:T(8,128)} copy(f32[8192,256]{1,0:T(8,128)S(1)} %shard_map.28) | data formatting | bytes 16777216

commit v3 on v2

--- a/solution.py
+++ b/solution.py
@@ -10,8 +10,18 @@
 MESH = pl.DeviceIdType.MESH
 N = 65536
 W = 2048
-CHUNK = 256
+FIRST = (2048, 2048)
+SECOND = (2048, 1024, 512, 256, 256)
+STEP = 256
 LANES = 128
+
+
+def spans(sizes, base):
+    out = []
+    for size in sizes:
+        out.append((base, size))
+        base += size
+    return out
 
 
 def exchange_kernel(rows, cols, x_ref, s64_ref, s2_ref, out_ref,
@@ -21,8 +31,9 @@
     r = lax.axis_index("row")
     c = lax.axis_index("col")
     local_rows, local_cols = x_ref.shape
-    count = local_rows // CHUNK
-    half = count // 2
+    half_rows = local_rows // 2
+    pieces1 = spans(FIRST, 0), spans(FIRST, half_rows)
+    pieces2 = spans(SECOND, 0), spans(SECOND, half_rows)
     top = r < rows // 2
     left = c < cols // 2
     z_peer = (lax.rem(r + rows // 2, rows), c)
@@ -30,21 +41,21 @@
     source_row = jnp.where(left, 0, rows // 2)
     is_source = r == source_row
 
-    def window(i):
-        return pl.ds(pl.multiple_of(i * CHUNK, CHUNK), CHUNK)
-
-    def load(i):
-        return pltpu.make_async_copy(x_ref.at[window(i)], mid.at[window(i)], load_sem.at[i])
-
-    def first(i, peer):
+    def load(half, i):
+        window = pl.ds(*pieces1[half][i])
+        return pltpu.make_async_copy(x_ref.at[window], mid.at[window], load_sem.at[half, i])
+
+    def first(half, i):
+        window = pl.ds(*pieces1[half][i])
         return pltpu.make_async_remote_copy(
-            x_ref.at[window(i)], got1.at[window(i)], send1.at[i], recv1.at[i],
-            device_id=peer, device_id_type=MESH)
-
-    def second(i, peer):
+            x_ref.at[window], got1.at[window], send1.at[half, i], recv1.at[half, i],
+            device_id=(z_peer, x_peer)[half], device_id_type=MESH)
+
+    def second(half, i):
+        window = pl.ds(*pieces2[half][i])
         return pltpu.make_async_remote_copy(
-            mid.at[window(i)], got2.at[window(i)], send2.at[i], recv2.at[i],
-            device_id=peer, device_id_type=MESH)
+            mid.at[window], got2.at[window], send2.at[half, i], recv2.at[half, i],
+            device_id=(x_peer, z_peer)[half], device_id_type=MESH)
 
     def scales(k):
         return pltpu.make_async_remote_copy(
@@ -60,14 +71,12 @@
         pl.semaphore_signal(ready, inc=1, device_id=peer, device_id_type=MESH)
 
     def send_z():
-        @pl.loop(0, half)
-        def _(i):
-            first(i, z_peer).start()
+        for i in range(len(FIRST)):
+            first(0, i).start()
 
     def send_x():
-        @pl.loop(half, count)
-        def _(i):
-            first(i, x_peer).start()
+        for i in range(len(FIRST)):
+            first(1, i).start()
 
     @pl.when(top)
     def _():
@@ -111,9 +120,9 @@
     load_scale = pltpu.make_async_copy(s64_ref, s64, scale_sem.at[0])
     load_scale.start()
 
-    @pl.loop(0, count)
-    def _(i):
-        load(i).start()
+    for i in range(len(FIRST)):
+        load(0, i).start()
+        load(1, i).start()
 
     load_scale.wait()
 
@@ -140,19 +149,23 @@
     z_sign = jnp.where(top, 1.0, -1.0).astype(jnp.float32)
     x_sign = jnp.where(left, 1.0, -1.0).astype(jnp.float32)
 
-    def mix(i, sign):
-        mid[window(i), :] = got1[window(i), :] + sign * mid[window(i), :]
-
-    @pl.loop(0, half)
-    def _(i):
-        load(i).wait()
-        first(i, z_peer).wait_recv()
-        mix(i, z_sign)
-        second(i, x_peer).start()
-        load(i + half).wait()
-        first(i + half, x_peer).wait_recv()
-        mix(i + half, x_sign)
-        second(i + half, z_peer).start()
+    first_sign = z_sign, x_sign
+    second_sign = x_sign, z_sign
+
+    for i in range(len(FIRST)):
+        for half in range(2):
+            base, size = pieces1[half][i]
+            load(half, i).wait()
+            first(half, i).wait_recv()
+
+            @pl.loop(0, size // STEP)
+            def _(t):
+                window = pl.ds(pl.multiple_of(base + t * STEP, STEP), STEP)
+                mid[window, :] = got1[window, :] + first_sign[half] * mid[window, :]
+
+            for j, (start, length) in enumerate(pieces2[half]):
+                if base < start + length <= base + size:
+                    second(half, j).start()
 
     @pl.when(is_source)
     def _():
@@ -166,34 +179,32 @@
 
     global_col = jnp.where(left, c * local_cols, N // 2 + c * local_cols - W)
 
-    def finish(i, sign):
-        base = r * local_rows + i * CHUNK
-        for b in range(local_cols // LANES):
-            lanes = slice(b * LANES, (b + 1) * LANES)
-            value = got2[window(i), lanes] + sign * mid[window(i), lanes]
-            value = value * (srow[window(i), :] * cscale[b : b + 1, :])
-            row_index = base + lax.broadcasted_iota(jnp.int32, (CHUNK, LANES), 0)
-            col_index = global_col + b * LANES + lax.broadcasted_iota(jnp.int32, (CHUNK, LANES), 1)
-            out_ref[window(i), lanes] = jnp.where(row_index >= col_index, value, jnp.float32(0.0))
-
-    @pl.loop(0, half)
-    def _(i):
-        second(i, x_peer).wait_recv()
-        finish(i, x_sign)
-        second(i + half, z_peer).wait_recv()
-        finish(i + half, z_sign)
-
-    @pl.loop(0, half)
-    def _(i):
-        first(i, z_peer).wait_send()
-        first(i + half, x_peer).wait_send()
-        second(i, x_peer).wait_send()
-        second(i + half, z_peer).wait_send()
+    for i in range(len(SECOND)):
+        for half in range(2):
+            base, size = pieces2[half][i]
+            second(half, i).wait_recv()
+
+            @pl.loop(0, size // STEP)
+            def _(t):
+                here = base + t * STEP
+                window = pl.ds(pl.multiple_of(here, STEP), STEP)
+                for b in range(local_cols // LANES):
+                    lanes = slice(b * LANES, (b + 1) * LANES)
+                    value = got2[window, lanes] + second_sign[half] * mid[window, lanes]
+                    value = value * (srow[window, :] * cscale[b : b + 1, :])
+                    row_index = r * local_rows + here + lax.broadcasted_iota(jnp.int32, value.shape, 0)
+                    col_index = global_col + b * LANES + lax.broadcasted_iota(jnp.int32, value.shape, 1)
+                    out_ref[window, lanes] = jnp.where(row_index >= col_index, value, jnp.float32(0.0))
+
+    for half in range(2):
+        for i in range(len(FIRST)):
+            first(half, i).wait_send()
+        for i in range(len(SECOND)):
+            second(half, i).wait_send()
 
 
 def per_device(rows, cols, slab_pair, butterfly_scale):
     local_rows, local_cols = slab_pair.shape
-    count = local_rows // CHUNK
     hbm = pl.BlockSpec(memory_space=pltpu.HBM)
     vmem = pl.BlockSpec(memory_space=pltpu.VMEM)
     s64 = butterfly_scale.reshape(local_rows // LANES, LANES)
@@ -210,7 +221,8 @@
             pltpu.VMEM((local_rows, LANES), jnp.float32),
             pltpu.VMEM((local_rows // LANES, LANES), jnp.float32),
             pltpu.VMEM((local_cols // LANES, LANES), jnp.float32),
-            dma((count,)), dma((count,)), dma((count,)), dma((count,)), dma((count,)),
+            dma((2, len(FIRST))), dma((2, len(FIRST))), dma((2, len(FIRST))),
+            dma((2, len(SECOND))), dma((2, len(SECOND))),
             dma((rows - 1,)), dma, dma((2,)),
             pltpu.SemaphoreType.REGULAR, pltpu.SemaphoreType.REGULAR,
         ],

time: 192 us -> 191 us (level)
  Pallas kernels: 189 us -> 187 us
where the time goes in v3:
time: 191 us
  Pallas kernels  187 us (98%)
  local copies, waits for them, and re-layouts  3.4 us (2%)
    pallas_call x1, Pallas kernels, per_device(): pl.pallas_call(functools.partial(exchange_kernel, rows, cols), out_shape=...  187 us

profile of v3, /device:TPU:6, one launch (start us, length us, event | category | flops | bytes accessed | tf_op | source)
XLA Modules:
  0.0 190.8 jit_solution(6081299680396862773)
XLA Ops:
  0.0 187.4 %shard_map.28 = f32[8192,256]{1,0:T(8,128)S(1)} custom-call(f32[8192,256]{1,0:T(8,128)} %x_ref.1, f32[64,128]{1,0:T(8,128)} %bitcast.2, f32[32,2,128]{2,1,0:T(2,128)} %bitcast.3), custom_call_target="tpu_custom_call" | custom-call | tf_op jit(solution)/shard_map/pallas_call | solution.py:214
  187.4 3.4 %copy.4 = f32[8192,256]{1,0:T(8,128)} copy(f32[8192,256]{1,0:T(8,128)S(1)} %shard_map.28) | data formatting | bytes 16777216

commit v4 on v3

--- a/solution.py
+++ b/solution.py
@@ -27,7 +27,7 @@
 def exchange_kernel(rows, cols, x_ref, s64_ref, s2_ref, out_ref,
                     mid, got1, got2, srow, s64, cscale,
                     load_sem, send1, recv1, send2, recv2, cs_send, cs_recv,
-                    scale_sem, ready_z, ready_x):
+                    scale_sem, ready_z, ready_x, all_in):
     r = lax.axis_index("row")
     c = lax.axis_index("col")
     local_rows, local_cols = x_ref.shape
@@ -38,23 +38,25 @@
     left = c < cols // 2
     z_peer = (lax.rem(r + rows // 2, rows), c)
     x_peer = (r, lax.rem(c + cols // 2, cols))
+    half_cols = cols // 2
     source_row = jnp.where(left, 0, rows // 2)
     is_source = r == source_row
+    hub = is_source & left
 
     def load(half, i):
         window = pl.ds(*pieces1[half][i])
-        return pltpu.make_async_copy(x_ref.at[window], mid.at[window], load_sem.at[half, i])
+        return pltpu.make_async_copy(x_ref.at[window], mid.at[window], load_sem.at[half])
 
     def first(half, i):
         window = pl.ds(*pieces1[half][i])
         return pltpu.make_async_remote_copy(
-            x_ref.at[window], got1.at[window], send1.at[half, i], recv1.at[half, i],
+            x_ref.at[window], got1.at[window], send1.at[half], recv1.at[half, i],
             device_id=(z_peer, x_peer)[half], device_id_type=MESH)
 
     def second(half, i):
         window = pl.ds(*pieces2[half][i])
         return pltpu.make_async_remote_copy(
-            mid.at[window], got2.at[window], send2.at[half, i], recv2.at[half, i],
+            mid.at[window], got2.at[window], send2.at[half], recv2.at[half, i],
             device_id=(x_peer, z_peer)[half], device_id_type=MESH)
 
     def scales(k):
@@ -86,16 +88,15 @@
     def _():
         greet(x_peer)
 
-    @pl.when(jnp.logical_not(is_source))
-    def _():
-        greet((source_row, c))
+    @pl.when(jnp.logical_not(hub))
+    def _():
+        greet((0, lax.rem(c, half_cols)))
 
     greetings = jnp.where(top, 0, 1) + jnp.where(left, 0, 1)
 
     @pl.when(greetings > 0)
     def _():
-        late_source = is_source & jnp.logical_not(left)
-        pl.semaphore_wait(barrier, greetings + jnp.where(late_source, rows - 1, 0))
+        pl.semaphore_wait(barrier, greetings)
 
     @pl.when(jnp.logical_not(top))
     def _():
@@ -131,16 +132,20 @@
         line = jnp.broadcast_to(s64[pl.ds(g, 1), :], (LANES, LANES))
         srow[pl.ds(pl.multiple_of(g * LANES, LANES), LANES), :] = line.T * jnp.float32(0.5)
 
-    own_scale = pltpu.make_async_copy(s2_ref.at[lax.rem(c, cols // 2)], cscale, scale_sem.at[1])
+    @pl.when(hub)
+    def _():
+        pl.semaphore_wait(barrier, 2 * rows - 1)
+        answer(all_in, (rows // 2, c + half_cols))
 
     @pl.when(is_source)
     def _():
+        own_scale = pltpu.make_async_copy(s2_ref.at[lax.rem(c, half_cols)], cscale, scale_sem.at[1])
         own_scale.start()
         own_scale.wait()
 
-        @pl.when(left)
+        @pl.when(jnp.logical_not(left))
         def _():
-            pl.semaphore_wait(barrier, rows - 1)
+            pl.semaphore_wait(all_in, 1)
 
         @pl.loop(0, rows - 1)
         def _(k):
@@ -155,7 +160,9 @@
     for i in range(len(FIRST)):
         for half in range(2):
             base, size = pieces1[half][i]
-            load(half, i).wait()
+            if i == 0:
+                whole = pl.ds(half * half_rows, half_rows)
+                pltpu.make_async_copy(x_ref.at[whole], mid.at[whole], load_sem.at[half]).wait()
             first(half, i).wait_recv()
 
             @pl.loop(0, size // STEP)
@@ -197,10 +204,11 @@
                     out_ref[window, lanes] = jnp.where(row_index >= col_index, value, jnp.float32(0.0))
 
     for half in range(2):
-        for i in range(len(FIRST)):
-            first(half, i).wait_send()
-        for i in range(len(SECOND)):
-            second(half, i).wait_send()
+        whole = pl.ds(half * half_rows, half_rows)
+        for source, sem, peer in ((x_ref, send1, (z_peer, x_peer)), (mid, send2, (x_peer, z_peer))):
+            pltpu.make_async_remote_copy(
+                source.at[whole], got1.at[whole], sem.at[half], recv1.at[half, 0],
+                device_id=peer[half], device_id_type=MESH).wait_send()
 
 
 def per_device(rows, cols, slab_pair, butterfly_scale):
@@ -221,10 +229,9 @@
             pltpu.VMEM((local_rows, LANES), jnp.float32),
             pltpu.VMEM((local_rows // LANES, LANES), jnp.float32),
             pltpu.VMEM((local_cols // LANES, LANES), jnp.float32),
-            dma((2, len(FIRST))), dma((2, len(FIRST))), dma((2, len(FIRST))),
-            dma((2, len(SECOND))), dma((2, len(SECOND))),
+            dma((2,)), dma((2,)), dma((2, len(FIRST))), dma((2,)), dma((2, len(SECOND))),
             dma((rows - 1,)), dma, dma((2,)),
-            pltpu.SemaphoreType.REGULAR, pltpu.SemaphoreType.REGULAR,
+            pltpu.SemaphoreType.REGULAR, pltpu.SemaphoreType.REGULAR, pltpu.SemaphoreType.REGULAR,
         ],
         compiler_params=pltpu.CompilerParams(
             collective_id=0, has_side_effects=True, vmem_limit_bytes=40 * 1024 * 1024

time: 191 us -> 190 us (level)
  no operation moved by 1% of the time
where the time goes in v4:
time: 190 us
  Pallas kernels  186 us (98%)
  local copies, waits for them, and re-layouts  3.4 us (2%)
    pallas_call x1, Pallas kernels, per_device(): pl.pallas_call(functools.partial(exchange_kernel, rows, cols), out_shape=...  186 us

profile of v4, /device:TPU:6, one launch (start us, length us, event | category | flops | bytes accessed | tf_op | source)
XLA Modules:
  0.0 189.5 jit_solution(5072615343431025857)
XLA Ops:
  0.0 186.1 %shard_map.28 = f32[8192,256]{1,0:T(8,128)S(1)} custom-call(f32[8192,256]{1,0:T(8,128)} %x_ref.1, f32[64,128]{1,0:T(8,128)} %bitcast.2, f32[32,2,128]{2,1,0:T(2,128)} %bitcast.3), custom_call_target="tpu_custom_call" | custom-call | tf_op jit(solution)/shard_map/pallas_call | solution.py:222
  186.1 3.4 %copy.4 = f32[8192,256]{1,0:T(8,128)} copy(f32[8192,256]{1,0:T(8,128)S(1)} %shard_map.28) | data formatting | bytes 16777216

commit v5 on v4

--- a/solution.py
+++ b/solution.py
@@ -10,7 +10,7 @@
 MESH = pl.DeviceIdType.MESH
 N = 65536
 W = 2048
-FIRST = (2048, 2048)
+FIRST = (256, 1792, 2048)
 SECOND = (2048, 1024, 512, 256, 256)
 STEP = 256
 LANES = 128
@@ -45,12 +45,13 @@
 
     def load(half, i):
         window = pl.ds(*pieces1[half][i])
-        return pltpu.make_async_copy(x_ref.at[window], mid.at[window], load_sem.at[half])
+        return pltpu.make_async_copy(x_ref.at[window], mid.at[window], load_sem.at[half, i])
 
     def first(half, i):
         window = pl.ds(*pieces1[half][i])
         return pltpu.make_async_remote_copy(
-            x_ref.at[window], got1.at[window], send1.at[half], recv1.at[half, i],
+            (x_ref if i else mid).at[window], got1.at[window],
+            send1.at[half, min(i, 1)], recv1.at[half, i],
             device_id=(z_peer, x_peer)[half], device_id_type=MESH)
 
     def second(half, i):
@@ -73,13 +74,18 @@
         pl.semaphore_signal(ready, inc=1, device_id=peer, device_id_type=MESH)
 
     def send_z():
+        load(0, 0).wait()
         for i in range(len(FIRST)):
             first(0, i).start()
 
     def send_x():
+        load(1, 0).wait()
         for i in range(len(FIRST)):
             first(1, i).start()
 
+    load(0, 0).start()
+    load(1, 0).start()
+
     @pl.when(top)
     def _():
         greet(z_peer)
@@ -101,13 +107,16 @@
     @pl.when(jnp.logical_not(top))
     def _():
         answer(ready_z, z_peer)
-        send_z()
 
     @pl.when(jnp.logical_not(left))
     def _():
         answer(ready_x, x_peer)
         send_x()
 
+    @pl.when(jnp.logical_not(top))
+    def _():
+        send_z()
+
     @pl.when(top)
     def _():
         pl.semaphore_wait(ready_z, 1)
@@ -121,7 +130,7 @@
     load_scale = pltpu.make_async_copy(s64_ref, s64, scale_sem.at[0])
     load_scale.start()
 
-    for i in range(len(FIRST)):
+    for i in range(1, len(FIRST)):
         load(0, i).start()
         load(1, i).start()
 
@@ -154,25 +163,30 @@
     z_sign = jnp.where(top, 1.0, -1.0).astype(jnp.float32)
     x_sign = jnp.where(left, 1.0, -1.0).astype(jnp.float32)
 
+    blank = top & jnp.logical_not(left)
+    needed = jnp.logical_not(top & left), top | left
     first_sign = z_sign, x_sign
     second_sign = x_sign, z_sign
 
     for i in range(len(FIRST)):
         for half in range(2):
             base, size = pieces1[half][i]
-            if i == 0:
-                whole = pl.ds(half * half_rows, half_rows)
-                pltpu.make_async_copy(x_ref.at[whole], mid.at[whole], load_sem.at[half]).wait()
             first(half, i).wait_recv()
+            if i:
+                load(half, i).wait()
+            else:
+                first(half, i).wait_send()
 
             @pl.loop(0, size // STEP)
             def _(t):
                 window = pl.ds(pl.multiple_of(base + t * STEP, STEP), STEP)
                 mid[window, :] = got1[window, :] + first_sign[half] * mid[window, :]
 
-            for j, (start, length) in enumerate(pieces2[half]):
-                if base < start + length <= base + size:
-                    second(half, j).start()
+            @pl.when(needed[half])
+            def _():
+                for j, (start, length) in enumerate(pieces2[half]):
+                    if base < start + length <= base + size:
+                        second(half, j).start()
 
     @pl.when(is_source)
     def _():
@@ -186,29 +200,43 @@
 
     global_col = jnp.where(left, c * local_cols, N // 2 + c * local_cols - W)
 
-    for i in range(len(SECOND)):
-        for half in range(2):
-            base, size = pieces2[half][i]
-            second(half, i).wait_recv()
-
-            @pl.loop(0, size // STEP)
-            def _(t):
-                here = base + t * STEP
-                window = pl.ds(pl.multiple_of(here, STEP), STEP)
-                for b in range(local_cols // LANES):
-                    lanes = slice(b * LANES, (b + 1) * LANES)
-                    value = got2[window, lanes] + second_sign[half] * mid[window, lanes]
-                    value = value * (srow[window, :] * cscale[b : b + 1, :])
-                    row_index = r * local_rows + here + lax.broadcasted_iota(jnp.int32, value.shape, 0)
-                    col_index = global_col + b * LANES + lax.broadcasted_iota(jnp.int32, value.shape, 1)
-                    out_ref[window, lanes] = jnp.where(row_index >= col_index, value, jnp.float32(0.0))
+    @pl.when(blank)
+    def _():
+        @pl.loop(0, local_rows // STEP)
+        def _(t):
+            out_ref[pl.ds(pl.multiple_of(t * STEP, STEP), STEP), :] = jnp.zeros((STEP, local_cols), jnp.float32)
+
+    @pl.when(jnp.logical_not(blank))
+    def _():
+        for i in range(len(SECOND)):
+            for half in range(2):
+                base, size = pieces2[half][i]
+                second(half, i).wait_recv()
+
+                @pl.loop(0, size // STEP)
+                def _(t):
+                    here = base + t * STEP
+                    window = pl.ds(pl.multiple_of(here, STEP), STEP)
+                    for b in range(local_cols // LANES):
+                        lanes = slice(b * LANES, (b + 1) * LANES)
+                        value = got2[window, lanes] + second_sign[half] * mid[window, lanes]
+                        value = value * (srow[window, :] * cscale[b : b + 1, :])
+                        row_index = r * local_rows + here + lax.broadcasted_iota(jnp.int32, value.shape, 0)
+                        col_index = global_col + b * LANES + lax.broadcasted_iota(jnp.int32, value.shape, 1)
+                        out_ref[window, lanes] = jnp.where(row_index >= col_index, value, jnp.float32(0.0))
+
+    def drained(source, base, size, sem):
+        window = pl.ds(base, size)
+        pltpu.make_async_remote_copy(
+            source.at[window], got1.at[window], sem, recv1.at[0, 0],
+            device_id=z_peer, device_id_type=MESH).wait_send()
 
     for half in range(2):
-        whole = pl.ds(half * half_rows, half_rows)
-        for source, sem, peer in ((x_ref, send1, (z_peer, x_peer)), (mid, send2, (x_peer, z_peer))):
-            pltpu.make_async_remote_copy(
-                source.at[whole], got1.at[whole], sem.at[half], recv1.at[half, 0],
-                device_id=peer[half], device_id_type=MESH).wait_send()
+        drained(x_ref, half * half_rows + FIRST[0], half_rows - FIRST[0], send1.at[half, 1])
+
+        @pl.when(needed[half])
+        def _():
+            drained(mid, half * half_rows, half_rows, send2.at[half])
 
 
 def per_device(rows, cols, slab_pair, butterfly_scale):
@@ -229,7 +257,7 @@
             pltpu.VMEM((local_rows, LANES), jnp.float32),
             pltpu.VMEM((local_rows // LANES, LANES), jnp.float32),
             pltpu.VMEM((local_cols // LANES, LANES), jnp.float32),
-            dma((2,)), dma((2,)), dma((2, len(FIRST))), dma((2,)), dma((2, len(SECOND))),
+            dma((2, len(FIRST))), dma((2, 2)), dma((2, len(FIRST))), dma((2,)), dma((2, len(SECOND))),
             dma((rows - 1,)), dma, dma((2,)),
             pltpu.SemaphoreType.REGULAR, pltpu.SemaphoreType.REGULAR, pltpu.SemaphoreType.REGULAR,
         ],

time: 190 us -> 189 us (level)
  no operation moved by 1% of the time
where the time goes in v5:
time: 189 us; the launch traced here: 188 us
  Pallas kernels  185 us (98%)
  local copies, waits for them, and re-layouts  3.4 us (2%)
    pallas_call x1, Pallas kernels, per_device(): pl.pallas_call(functools.partial(exchange_kernel, rows, cols), out_shape=...  185 us

profile of v5, /device:TPU:6, one launch (start us, length us, event | category | flops | bytes accessed | tf_op | source)
XLA Modules:
  0.0 188.5 jit_solution(13136850923227923623)
XLA Ops:
  0.0 185.1 %shard_map.28 = f32[8192,256]{1,0:T(8,128)S(1)} custom-call(f32[8192,256]{1,0:T(8,128)} %x_ref.1, f32[64,128]{1,0:T(8,128)} %bitcast.2, f32[32,2,128]{2,1,0:T(2,128)} %bitcast.3), custom_call_target="tpu_custom_call" | custom-call | tf_op jit(solution)/shard_map/pallas_call | solution.py:250
  185.1 3.4 %copy.4 = f32[8192,256]{1,0:T(8,128)} copy(f32[8192,256]{1,0:T(8,128)S(1)} %shard_map.28) | data formatting | bytes 16777216

commit v6 on v4

--- a/solution.py
+++ b/solution.py
@@ -10,9 +10,9 @@
 MESH = pl.DeviceIdType.MESH
 N = 65536
 W = 2048
-FIRST = (2048, 2048)
-SECOND = (2048, 1024, 512, 256, 256)
-STEP = 256
+FIRST = (128, 1920, 2048)
+SECOND = (2048, 1536, 384, 128)
+STEP = 128
 LANES = 128
 
 
@@ -45,12 +45,13 @@
 
     def load(half, i):
         window = pl.ds(*pieces1[half][i])
-        return pltpu.make_async_copy(x_ref.at[window], mid.at[window], load_sem.at[half])
+        return pltpu.make_async_copy(x_ref.at[window], mid.at[window], load_sem.at[half, i])
 
     def first(half, i):
         window = pl.ds(*pieces1[half][i])
         return pltpu.make_async_remote_copy(
-            x_ref.at[window], got1.at[window], send1.at[half], recv1.at[half, i],
+            (x_ref if i else mid).at[window], got1.at[window],
+            send1.at[half, min(i, 1)], recv1.at[half, i],
             device_id=(z_peer, x_peer)[half], device_id_type=MESH)
 
     def second(half, i):
@@ -73,13 +74,18 @@
         pl.semaphore_signal(ready, inc=1, device_id=peer, device_id_type=MESH)
 
     def send_z():
+        load(0, 0).wait()
         for i in range(len(FIRST)):
             first(0, i).start()
 
     def send_x():
+        load(1, 0).wait()
         for i in range(len(FIRST)):
             first(1, i).start()
 
+    load(0, 0).start()
+    load(1, 0).start()
+
     @pl.when(top)
     def _():
         greet(z_peer)
@@ -101,13 +107,16 @@
     @pl.when(jnp.logical_not(top))
     def _():
         answer(ready_z, z_peer)
-        send_z()
 
     @pl.when(jnp.logical_not(left))
     def _():
         answer(ready_x, x_peer)
         send_x()
 
+    @pl.when(jnp.logical_not(top))
+    def _():
+        send_z()
+
     @pl.when(top)
     def _():
         pl.semaphore_wait(ready_z, 1)
@@ -121,7 +130,7 @@
     load_scale = pltpu.make_async_copy(s64_ref, s64, scale_sem.at[0])
     load_scale.start()
 
-    for i in range(len(FIRST)):
+    for i in range(1, len(FIRST)):
         load(0, i).start()
         load(1, i).start()
 
@@ -160,10 +169,11 @@
     for i in range(len(FIRST)):
         for half in range(2):
             base, size = pieces1[half][i]
-            if i == 0:
-                whole = pl.ds(half * half_rows, half_rows)
-                pltpu.make_async_copy(x_ref.at[whole], mid.at[whole], load_sem.at[half]).wait()
             first(half, i).wait_recv()
+            if i:
+                load(half, i).wait()
+            else:
+                first(half, i).wait_send()
 
             @pl.loop(0, size // STEP)
             def _(t):
@@ -203,12 +213,15 @@
                     col_index = global_col + b * LANES + lax.broadcasted_iota(jnp.int32, value.shape, 1)
                     out_ref[window, lanes] = jnp.where(row_index >= col_index, value, jnp.float32(0.0))
 
+    def drained(source, base, size, sem):
+        window = pl.ds(base, size)
+        pltpu.make_async_remote_copy(
+            source.at[window], got1.at[window], sem, recv1.at[0, 0],
+            device_id=z_peer, device_id_type=MESH).wait_send()
+
     for half in range(2):
-        whole = pl.ds(half * half_rows, half_rows)
-        for source, sem, peer in ((x_ref, send1, (z_peer, x_peer)), (mid, send2, (x_peer, z_peer))):
-            pltpu.make_async_remote_copy(
-                source.at[whole], got1.at[whole], sem.at[half], recv1.at[half, 0],
-                device_id=peer[half], device_id_type=MESH).wait_send()
+        drained(x_ref, half * half_rows + FIRST[0], half_rows - FIRST[0], send1.at[half, 1])
+        drained(mid, half * half_rows, half_rows, send2.at[half])
 
 
 def per_device(rows, cols, slab_pair, butterfly_scale):
@@ -229,7 +242,7 @@
             pltpu.VMEM((local_rows, LANES), jnp.float32),
             pltpu.VMEM((local_rows // LANES, LANES), jnp.float32),
             pltpu.VMEM((local_cols // LANES, LANES), jnp.float32),
-            dma((2,)), dma((2,)), dma((2, len(FIRST))), dma((2,)), dma((2, len(SECOND))),
+            dma((2, len(FIRST))), dma((2, 2)), dma((2, len(FIRST))), dma((2,)), dma((2, len(SECOND))),
             dma((rows - 1,)), dma, dma((2,)),
             pltpu.SemaphoreType.REGULAR, pltpu.SemaphoreType.REGULAR, pltpu.SemaphoreType.REGULAR,
         ],

time: 190 us -> 189 us (level)
  no operation moved by 1% of the time
where the time goes in v6:
time: 189 us
  Pallas kernels  186 us (98%)
  local copies, waits for them, and re-layouts  3.4 us (2%)
    pallas_call x1, Pallas kernels, per_device(): pl.pallas_call(functools.partial(exchange_kernel, rows, cols), out_shape=...  186 us

profile of v6, /device:TPU:6, one launch (start us, length us, event | category | flops | bytes accessed | tf_op | source)
XLA Modules:
  0.0 189.3 jit_solution(15373419376584961659)
XLA Ops:
  0.0 185.9 %shard_map.28 = f32[8192,256]{1,0:T(8,128)S(1)} custom-call(f32[8192,256]{1,0:T(8,128)} %x_ref.1, f32[64,128]{1,0:T(8,128)} %bitcast.2, f32[32,2,128]{2,1,0:T(2,128)} %bitcast.3), custom_call_target="tpu_custom_call" | custom-call | tf_op jit(solution)/shard_map/pallas_call | solution.py:235
  185.9 3.4 %copy.4 = f32[8192,256]{1,0:T(8,128)} copy(f32[8192,256]{1,0:T(8,128)S(1)} %shard_map.28) | data formatting | bytes 16777216

commit v7 on v6

--- a/solution.py
+++ b/solution.py
@@ -11,7 +11,7 @@
 N = 65536
 W = 2048
 FIRST = (128, 1920, 2048)
-SECOND = (2048, 1536, 384, 128)
+SECOND = (2048, 1792, 256)
 STEP = 128
 LANES = 128
 
@@ -45,7 +45,7 @@
 
     def load(half, i):
         window = pl.ds(*pieces1[half][i])
-        return pltpu.make_async_copy(x_ref.at[window], mid.at[window], load_sem.at[half, i])
+        return pltpu.make_async_copy(x_ref.at[window], mid.at[window], load_sem.at[half, min(i, 1)])
 
     def first(half, i):
         window = pl.ds(*pieces1[half][i])
@@ -62,7 +62,7 @@
 
     def scales(k):
         return pltpu.make_async_remote_copy(
-            cscale, cscale, cs_send.at[k], cs_recv,
+            cscale, cscale, cs_send, cs_recv,
             device_id=(lax.rem(source_row + 1 + k, rows), c), device_id_type=MESH)
 
     barrier = pltpu.get_barrier_semaphore()
@@ -127,7 +127,7 @@
         pl.semaphore_wait(ready_x, 1)
         send_x()
 
-    load_scale = pltpu.make_async_copy(s64_ref, s64, scale_sem.at[0])
+    load_scale = pltpu.make_async_copy(s64_ref, s64, scale_sem)
     load_scale.start()
 
     for i in range(1, len(FIRST)):
@@ -148,7 +148,7 @@
 
     @pl.when(is_source)
     def _():
-        own_scale = pltpu.make_async_copy(s2_ref.at[lax.rem(c, half_cols)], cscale, scale_sem.at[1])
+        own_scale = pltpu.make_async_copy(s2_ref.at[lax.rem(c, half_cols)], cscale, scale_sem)
         own_scale.start()
         own_scale.wait()
 
@@ -170,9 +170,10 @@
         for half in range(2):
             base, size = pieces1[half][i]
             first(half, i).wait_recv()
-            if i:
-                load(half, i).wait()
-            else:
+            if i == 1:
+                rest = pl.ds(half * half_rows + FIRST[0], half_rows - FIRST[0])
+                pltpu.make_async_copy(x_ref.at[rest], mid.at[rest], load_sem.at[half, 1]).wait()
+            elif i == 0:
                 first(half, i).wait_send()
 
             @pl.loop(0, size // STEP)
@@ -186,9 +187,9 @@
 
     @pl.when(is_source)
     def _():
-        @pl.loop(0, rows - 1)
-        def _(k):
-            scales(k).wait_send()
+        sent = srow.at[pl.ds(0, (rows - 1) * (local_cols // LANES))]
+        pltpu.make_async_remote_copy(
+            sent, sent, cs_send, cs_recv, device_id=z_peer, device_id_type=MESH).wait_send()
 
     @pl.when(jnp.logical_not(is_source))
     def _():
@@ -242,8 +243,8 @@
             pltpu.VMEM((local_rows, LANES), jnp.float32),
             pltpu.VMEM((local_rows // LANES, LANES), jnp.float32),
             pltpu.VMEM((local_cols // LANES, LANES), jnp.float32),
-            dma((2, len(FIRST))), dma((2, 2)), dma((2, len(FIRST))), dma((2,)), dma((2, len(SECOND))),
-            dma((rows - 1,)), dma, dma((2,)),
+            dma((2, 2)), dma((2, 2)), dma((2, len(FIRST))), dma((2,)), dma((2, len(SECOND))),
+            dma, dma, dma,
             pltpu.SemaphoreType.REGULAR, pltpu.SemaphoreType.REGULAR, pltpu.SemaphoreType.REGULAR,
         ],
         compiler_params=pltpu.CompilerParams(

time: 189 us -> 189 us (level)
  no operation moved by 1% of the time
where the time goes in v7:
time: 189 us
  Pallas kernels  186 us (98%)
  local copies, waits for them, and re-layouts  3.4 us (2%)
    pallas_call x1, Pallas kernels, per_device(): pl.pallas_call(functools.partial(exchange_kernel, rows, cols), out_shape=...  186 us

profile of v7, /device:TPU:6, one launch (start us, length us, event | category | flops | bytes accessed | tf_op | source)
XLA Modules:
  0.0 189.3 jit_solution(6951465952066138093)
XLA Ops:
  0.0 185.9 %shard_map.28 = f32[8192,256]{1,0:T(8,128)S(1)} custom-call(f32[8192,256]{1,0:T(8,128)} %x_ref.1, f32[64,128]{1,0:T(8,128)} %bitcast.2, f32[32,2,128]{2,1,0:T(2,128)} %bitcast.3), custom_call_target="tpu_custom_call" | custom-call | tf_op jit(solution)/shard_map/pallas_call | solution.py:236
  185.9 3.4 %copy.4 = f32[8192,256]{1,0:T(8,128)} copy(f32[8192,256]{1,0:T(8,128)S(1)} %shard_map.28) | data formatting | bytes 16777216

commit v8 on v7

--- a/solution.py
+++ b/solution.py
@@ -14,6 +14,7 @@
 SECOND = (2048, 1792, 256)
 STEP = 128
 LANES = 128
+PARTS = 16
 
 
 def spans(sizes, base):
@@ -233,7 +234,7 @@
     s2 = butterfly_scale.reshape(local_rows // local_cols, local_cols // LANES, LANES)
     block = pltpu.VMEM((local_rows, local_cols), jnp.float32)
     dma = pltpu.SemaphoreType.DMA
-    return pl.pallas_call(
+    mixed = pl.pallas_call(
         functools.partial(exchange_kernel, rows, cols),
         out_shape=jax.ShapeDtypeStruct(slab_pair.shape, slab_pair.dtype),
         in_specs=[hbm, hbm, hbm],
@@ -252,6 +253,21 @@
         ),
     )(slab_pair, *(pltpu.with_memory_space_constraint(s, pltpu.HBM) for s in (s64, s2)))
 
+    def write_out(from_ref, to_ref, sem):
+        for k in range(PARTS):
+            window = pl.ds(k * (local_rows // PARTS), local_rows // PARTS)
+            pltpu.make_async_copy(from_ref.at[window], to_ref.at[window], sem).start()
+        pltpu.make_async_copy(from_ref, to_ref, sem).wait()
+
+    return pl.pallas_call(
+        write_out,
+        out_shape=jax.ShapeDtypeStruct(slab_pair.shape, slab_pair.dtype),
+        in_specs=[vmem],
+        out_specs=hbm,
+        scratch_shapes=[dma],
+        compiler_params=pltpu.CompilerParams(vmem_limit_bytes=1024 * 1024),
+    )(mixed)
+
 
 def solution(mesh):
     return jax.shard_map(

time: 189 us -> 189 us (level)
  local copies, waits for them, and re-layouts: 3.4 us -> 0 us
  Pallas kernels: 186 us -> 189 us
    unnamed x1 -> x0, local copies, waits for them, and re-layouts: 3.4 us -> none
    pallas_call x0 -> x1, Pallas kernels: none -> 3.28 us  [per_device(): pl.pallas_call(write_out, out_shape=jax.ShapeDtypeStruct(slab_pair.shape,...]
where the time goes in v8:
time: 189 us
  Pallas kernels  189 us (100%)
    pallas_call x1, Pallas kernels, per_device(): pl.pallas_call(functools.partial(exchange_kernel, rows, cols), out_shape=...  186 us

profile of v8, /device:TPU:6, one launch (start us, length us, event | category | flops | bytes accessed | tf_op | source)
XLA Modules:
  0.0 189.2 jit_solution(17090886808602060467)
XLA Ops:
  0.0 185.9 %shard_map.28.from_ref = f32[8192,256]{1,0:T(8,128)S(1)} custom-call(f32[8192,256]{1,0:T(8,128)} %x_ref.1, f32[64,128]{1,0:T(8,128)} %bitcast.2, f32[32,2,128]{2,1,0:T(2,128)} %bitcast.3), custom_call_target="tpu_custom_call" | custom-call | tf_op jit(solution)/shard_map/pallas_call | solution.py:237
  185.9 3.3 %shard_map.29 = f32[8192,256]{1,0:T(8,128)} custom-call(f32[8192,256]{1,0:T(8,128)S(1)} %shard_map.28.from_ref), custom_call_target="tpu_custom_call" | custom-call | tf_op jit(solution)/shard_map/pallas_call | solution.py:262

commit v9 on v8

--- a/solution.py
+++ b/solution.py
@@ -14,7 +14,7 @@
 SECOND = (2048, 1792, 256)
 STEP = 128
 LANES = 128
-PARTS = 16
+PARTS = 32
 
 
 def spans(sizes, base):

time: 189 us -> 189 us (level)
  no operation moved by 1% of the time
where the time goes in v9:
time: 189 us
  Pallas kernels  189 us (100%)
    pallas_call x1, Pallas kernels, per_device(): pl.pallas_call(functools.partial(exchange_kernel, rows, cols), out_shape=...  186 us

profile of v9, /device:TPU:6, one launch (start us, length us, event | category | flops | bytes accessed | tf_op | source)
XLA Modules:
  0.0 189.1 jit_solution(1049112849325092614)
XLA Ops:
  0.0 185.9 %shard_map.28.from_ref = f32[8192,256]{1,0:T(8,128)S(1)} custom-call(f32[8192,256]{1,0:T(8,128)} %x_ref.1, f32[64,128]{1,0:T(8,128)} %bitcast.2, f32[32,2,128]{2,1,0:T(2,128)} %bitcast.3), custom_call_target="tpu_custom_call" | custom-call | tf_op jit(solution)/shard_map/pallas_call | solution.py:237
  185.9 3.3 %shard_map.29 = f32[8192,256]{1,0:T(8,128)} custom-call(f32[8192,256]{1,0:T(8,128)S(1)} %shard_map.28.from_ref), custom_call_target="tpu_custom_call" | custom-call | tf_op jit(solution)/shard_map/pallas_call | solution.py:262
